TPU v7x, 32 devices: a whole 2x2x4 slice. The times are simulated.
32 devices in a mesh: runs: 2 (over y), gx: 4 (over z), gy: 2 (over x), gz: 2 (over core).
Axes of the slice: x: 2, y: 2, z: 4, core: 2. Of those that a mesh axis runs over, the one named last changes fastest.
Arguments:
- positions: float32 [3, 8, 4096], P(None, None, ('runs', 'gx', 'gy', 'gz')), parts along dimension 2, as said below
- velocities: float32 [3, 8, 4096], P(None, None, ('runs', 'gx', 'gy', 'gz')), parts along dimension 2, may hold values from -5 to 5
- send_list: int32 [5696], P(('runs', 'gx', 'gy', 'gz')), parts along dimension 0, may hold values from 0 to 127
- pair_list: int32 [2, 57344], P(None, ('runs', 'gx', 'gy', 'gz')), parts along dimension 1, may hold values from 0 to 306, as said below
- constraint_flags: int32 [7, 4096], P(None, ('runs', 'gx', 'gy', 'gz')), parts along dimension 1, may hold values 0 or 1
Outputs:
- final_positions: float32 [3, 8, 4096], P(None, None, ('runs', 'gx', 'gy', 'gz')), parts along dimension 2
- final_velocities: float32 [3, 8, 4096], P(None, None, ('runs', 'gx', 'gy', 'gz')), parts along dimension 2
- energies: float32 [6, 2], P('runs'), parts along dimension 0
There are 2 independent parts, one for each index of `runs`. A program takes and returns all parts, laid end to end along the dimension named above; each array names one. Nothing has to cross between parts.
Inputs may be any that keep to these rules, and one draw needn't show every extreme that they name: `pair_list`: each domain's 1792 slots name clusters of its extended set: 0 to 127 its own, then its received zone blocks in order; padding slots hold 306 in both rows; every cluster appears in a slot with itself; no unordered pair appears twice. `positions`: eight beads of a cluster lie in its cell of side 1, the cells of a domain filling a box of 1 by 8 by 16; neighbouring beads of a cluster are between 0.25 and 0.6 apart.
All inputs are finite; a program needn't handle non-finite values. No bound on the sum of `constraint_flags` on one device may be relied on, other than what follows from the above.
Results may differ from a plain program's by a relative error of at most 0.0003.
Values sent between devices are 32-bit elements; how exact they have to be, the bound alone decides.
A program may use at most 64 MiB of HBM per device.

v0:
```python
import jax
import jax.numpy as jnp
import numpy as np
from jax import lax
from jax.sharding import PartitionSpec as P

CX = 1
CY = 8
CZ = 16
ITERS = 3
NORDER = 4
time_step = 0.02
strength = 2.0
root_half = 0.7071067811865476
zone_list = ((1, 0, 0), (0, 1, 0), (0, 0, 1), (1, 1, 0), (1, 0, 1), (0, 1, 1), (1, 1, 1))


def from_behind(value, axis, by):
    count = lax.axis_size(axis)
    return lax.ppermute(value, axis, [(i, (i + by) % count) for i in range(count)])


def zone_sizes():
    return tuple(
        (
            (CX if direction[0] == 0 else 1)
            * (CY if direction[1] == 0 else 1)
            * (CZ if direction[2] == 0 else 1)
            for direction in zone_list
        )
    )


def split_blocks(packed, block_sizes):
    pieces = []
    position = 0
    for length in block_sizes:
        pieces.append(packed[:, :, position : position + length])
        position += length
    return pieces


def shell_offsets():
    block_sizes = zone_sizes()
    columns = []
    for number in range(7):
        direction = zone_list[number]
        column = np.array(
            [[direction[0] * CX], [direction[1] * CY], [direction[2] * CZ]], np.float32
        )
        columns.append(np.tile(column, (1, block_sizes[number])))
    return jnp.asarray(np.concatenate(columns, axis=1))[:, None, :]


def share_coords(coords, send_list):
    sizes_all = zone_sizes()
    outgoing = split_blocks(jnp.take(coords, send_list, axis=2), sizes_all)
    along_y = from_behind(
        jnp.concatenate([outgoing[1], outgoing[3], outgoing[5], outgoing[6]], axis=2), "gy", -1
    )
    got_y = split_blocks(along_y, [sizes_all[1], sizes_all[3], sizes_all[5], sizes_all[6]])
    along_x = from_behind(
        jnp.concatenate([outgoing[0], outgoing[4], got_y[1], got_y[3]], axis=2), "gx", -1
    )
    got_x = split_blocks(along_x, [sizes_all[0], sizes_all[4], sizes_all[3], sizes_all[6]])
    along_z = from_behind(
        jnp.concatenate([outgoing[2], got_x[1], got_y[2], got_x[3]], axis=2), "gz", -1
    )
    got_z = split_blocks(along_z, [sizes_all[2], sizes_all[4], sizes_all[5], sizes_all[6]])
    received = [got_x[0], got_y[0], got_z[0], got_x[2], got_z[1], got_z[2], got_z[3]]
    return jnp.concatenate(received, axis=2) + shell_offsets()


def return_forces(halo_forces):
    sizes_all = zone_sizes()
    outgoing = split_blocks(halo_forces, sizes_all)
    along_z = from_behind(
        jnp.concatenate([outgoing[2], outgoing[4], outgoing[5], outgoing[6]], axis=2), "gz", 1
    )
    got_z = split_blocks(along_z, [sizes_all[2], sizes_all[4], sizes_all[5], sizes_all[6]])
    along_x = from_behind(
        jnp.concatenate([outgoing[0], outgoing[3], got_z[1], got_z[3]], axis=2), "gx", 1
    )
    got_x = split_blocks(along_x, [sizes_all[0], sizes_all[3], sizes_all[4], sizes_all[6]])
    settled = [got_x[0], got_z[0], got_x[2]]
    pending = [got_x[1], got_z[2], got_x[3]]
    along_y = from_behind(
        jnp.concatenate([outgoing[1], pending[0], pending[1], pending[2]], axis=2), "gy", 1
    )
    got_y = split_blocks(along_y, [sizes_all[1], sizes_all[3], sizes_all[5], sizes_all[6]])
    return jnp.concatenate(
        [settled[0], got_y[0], settled[1], got_y[1], settled[2], got_y[2], got_y[3]], axis=2
    )


def pair_tables(pair_list, extended_count):
    rows = lax.broadcasted_iota(jnp.int32, (extended_count, pair_list.shape[1]), 0)
    first_table = (rows == pair_list[0][None, :]).astype(jnp.float32)
    second_table = (rows == pair_list[1][None, :]).astype(jnp.float32)
    return (first_table, second_table)


def domain_forces(extended, pair_list, tables):
    extended_count = extended.shape[2]
    slot_count = pair_list.shape[1]
    first_ids = pair_list[0]
    second_ids = pair_list[1]
    flat = extended.reshape(24, extended_count)
    first_coords = jnp.dot(flat, tables[0], precision=lax.Precision.HIGHEST).reshape(
        3, 8, slot_count
    )
    second_coords = jnp.dot(flat, tables[1], precision=lax.Precision.HIGHEST).reshape(
        3, 8, slot_count
    )
    separation = first_coords[:, :, None, :] - second_coords[:, None, :, :]
    scaled = jnp.sum(separation * separation, axis=0)
    intersect = jnp.maximum(1.0 - scaled, 0.0)
    bead_row = lax.broadcasted_iota(jnp.int32, (8, 8, 1), 0)
    bead_column = lax.broadcasted_iota(jnp.int32, (8, 8, 1), 1)
    self_pair = (first_ids == second_ids)[None, None, :]
    usable = (first_ids < extended_count - 1)[None, None, :]
    weight = (jnp.where(self_pair, bead_row < bead_column, True) & usable).astype(jnp.float32)
    energy = strength * jnp.sum(weight * intersect * intersect * intersect)
    magnitude = 6.0 * strength * weight * intersect * intersect
    pushing = magnitude[None] * separation
    on_first = jnp.sum(pushing, axis=2).reshape(24, slot_count)
    on_second = (-jnp.sum(pushing, axis=1)).reshape(24, slot_count)
    contract = (((1,), (1,)), ((), ()))
    forces = lax.dot_general(on_first, tables[0], contract, precision=lax.Precision.HIGHEST)
    forces = forces + lax.dot_general(
        on_second, tables[1], contract, precision=lax.Precision.HIGHEST
    )
    return (forces.reshape(3, 8, extended_count), energy)


def local_forces(coords, send_list, pair_list, tables):
    halo_coords = share_coords(coords, send_list)
    dummy_cluster = jnp.zeros((3, 8, 1), jnp.float32)
    extended = jnp.concatenate([coords, halo_coords, dummy_cluster], axis=2)
    forces, energy = domain_forces(extended, pair_list, tables)
    cluster_count = coords.shape[2]
    returned = return_forces(forces[:, :, cluster_count : cluster_count + send_list.shape[0]])
    home_forces = forces[:, :, :cluster_count].at[:, :, send_list].add(returned)
    return (home_forces, energy)


def link_vectors(coords):
    return coords[:, :-1, :] - coords[:, 1:, :]


def link_lengths(coords):
    vectors = link_vectors(coords)
    return jnp.sqrt(jnp.sum(vectors * vectors, axis=0))


def expand(coupling, source):
    coupling_down = jnp.pad(coupling, ((1, 0), (0, 0)))
    coupling_up = jnp.pad(coupling, ((0, 1), (0, 0)))
    series = source
    result = source
    for expansion in range(NORDER):
        series = (
            coupling_down * jnp.pad(series, ((1, 0), (0, 0)))[:-1]
            + coupling_up * jnp.pad(series, ((0, 1), (0, 0)))[1:]
        )
        result = result + series
    return result


def apply_links(coords, directions, solution):
    shifts = directions * (root_half * solution)[None]
    return (
        coords
        - jnp.pad(shifts, ((0, 0), (0, 1), (0, 0)))
        + jnp.pad(shifts, ((0, 0), (1, 0), (0, 0)))
    )


def constrain(previous, updated, rest_length, link_flags):
    old_vectors = link_vectors(previous)
    directions = (
        old_vectors / jnp.maximum(jnp.sqrt(jnp.sum(old_vectors * old_vectors, axis=0)), 0.2)[None]
    )
    coupling = (
        0.5
        * jnp.sum(directions[:, :-1] * directions[:, 1:], axis=0)
        * link_flags[:-1]
        * link_flags[1:]
    )
    projected = jnp.sum(directions * link_vectors(updated), axis=0)
    solution = expand(coupling, link_flags * root_half * (projected - rest_length))
    updated = apply_links(updated, directions, solution)
    vectors = link_vectors(updated)
    squared = jnp.sum(vectors * vectors, axis=0)
    target = jnp.sqrt(
        jnp.maximum(2.0 * rest_length * rest_length - squared, 0.25 * rest_length * rest_length)
    )
    solution = expand(coupling, link_flags * root_half * (rest_length - target))
    updated = apply_links(updated, directions, solution)
    return updated


def on_device(positions, velocities, send_list, pair_list, constraint_flags):
    link_flags = constraint_flags.astype(jnp.float32)
    rest_length = link_lengths(positions)
    bead_total = 8 * positions.shape[2] * lax.axis_size(("gx", "gy", "gz"))
    tables = pair_tables(pair_list, positions.shape[2] + send_list.shape[0] + 1)
    forces, potential = local_forces(positions, send_list, pair_list, tables)
    energy_rows = []
    for iteration in range(ITERS):
        half_speed = velocities + 0.5 * time_step * forces
        updated = constrain(positions, positions + time_step * half_speed, rest_length, link_flags)
        half_speed = (updated - positions) / time_step
        forces, potential = local_forces(updated, send_list, pair_list, tables)
        velocities = half_speed + 0.5 * time_step * forces
        positions = updated
        kinetic = 0.5 * jnp.sum(velocities * velocities)
        energy_rows.append(jnp.stack([potential, kinetic]))
    energies = jnp.stack(energy_rows)
    energies = lax.psum(energies, ("gx", "gy", "gz"))
    return (positions, velocities, energies / bead_total)


def solution(mesh):
    return jax.shard_map(
        on_device,
        mesh=mesh,
        in_specs=(
            P(None, None, ("runs", "gx", "gy", "gz")),
            P(None, None, ("runs", "gx", "gy", "gz")),
            P(("runs", "gx", "gy", "gz")),
            P(None, ("runs", "gx", "gy", "gz")),
            P(None, ("runs", "gx", "gy", "gz")),
        ),
        out_specs=(
            P(None, None, ("runs", "gx", "gy", "gz")),
            P(None, None, ("runs", "gx", "gy", "gz")),
            P("runs", None),
        ),
        check_vma=False,
    )
```

profile of v0, /device:TPU:0, one launch (start us, length us, event | category | flops | bytes accessed | tf_op | source)
XLA Modules:
  0.0 178.5 jit_solution(6793706241259081876)
XLA Ops:
  4.1 3.0 %collective-permute-start = (f32[3,8,34]{2,1,0:T(8,128)S(1)}, f32[3,8,34]{2,1,0:T(8,128)S(1)}, u32[]{:S(2)}, u32[]{:S(2)}) collective-permute-start(f32[3,8,34]{2,1,0:T(8,128)S(1)} %pad_maximum_fusion.8), channel_id=1, source_target_pairs={{0,2},{2,0},{1,3},{3,1},{4,6},{6,4},{5,7},{7,5},{8,10},{10,8},{9,1... | collective-permute-start | bytes 9800 | tf_op jit(solution)/shard_map/ppermute | solution.py:20
  7.2 1.5 collective-permute-done
  9.0 4.1 %collective-permute-start.1 = (f32[3,8,153]{2,1,0:T(8,128)S(1)}, f32[3,8,153]{2,1,0:T(8,128)S(1)}, u32[]{:S(2)}, u32[]{:S(2)}) collective-permute-start(f32[3,8,153]{2,1,0:T(8,128)S(1)} %pad_maximum_fusion), channel_id=1, source_target_pairs={{0,12},{4,0},{8,4},{12,8},{1,13},{5,1},{9,5},{13,9},{2,14},{6,2},{... | collective-permute-start | bytes 44072 | tf_op jit(solution)/shard_map/ppermute | solution.py:20
  13.2 1.5 collective-permute-done.1
  18.8 1.1 fusion.3
  19.9 1.1 fusion.55
  23.0 5.6 %collective-permute-done.4 = f32[3,8,153]{2,1,0:T(8,128)S(1)} collective-permute-done((f32[3,8,153]{2,1,0:T(8,128)S(1)}, f32[3,8,153]{2,1,0:T(8,128)S(1)}, u32[]{:S(2)}, u32[]{:S(2)}) %collective-permute-start.4) | collective-permute-done | bytes 14720 | tf_op jit(solution)/shard_map/ppermute | solution.py:20
  28.7 1.5 collective-permute-start.5
  30.5 2.0 %collective-permute-done.5 = f32[3,8,34]{2,1,0:T(8,128)S(1)} collective-permute-done((f32[3,8,34]{2,1,0:T(8,128)S(1)}, f32[3,8,34]{2,1,0:T(8,128)S(1)}, u32[]{:S(2)}, u32[]{:S(2)}) %collective-permute-start.5) | collective-permute-done | bytes 3296 | tf_op jit(solution)/shard_map/ppermute | solution.py:20
  32.9 7.2 %scatter_fusion = f32[3,8,128]{1,0,2:T(4,128)S(1)} fusion(f32[3,8,128]{1,0,2:T(4,128)S(1)} %copy.120, s32[178]{0:T(256)S(1)} %compare_select_fusion, f32[178,3,8]{2,1,0:T(4,128)S(1)} %copy.102), kind=kCustom, calls=%fused_computation.4 | custom fusion | flops 4272 | bytes 51976 | tf_op jit(solution)/shard_map/scatter-add | solution.py:143
  41.9 1.5 collective-permute-start.6
  43.4 2.1 %collective-permute-done.6 = f32[3,8,34]{2,1,0:T(8,128)S(1)} collective-permute-done((f32[3,8,34]{2,1,0:T(8,128)S(1)}, f32[3,8,34]{2,1,0:T(8,128)S(1)}, u32[]{:S(2)}, u32[]{:S(2)}) %collective-permute-start.6) | collective-permute-done | bytes 3296 | tf_op jit(solution)/shard_map/ppermute | solution.py:20
  45.8 2.0 %collective-permute-start.7 = (f32[3,8,153]{2,1,0:T(8,128)S(1)}, f32[3,8,153]{2,1,0:T(8,128)S(1)}, u32[]{:S(2)}, u32[]{:S(2)}) collective-permute-start(f32[3,8,153]{2,1,0:T(8,128)S(1)} %pad_maximum_fusion.2), channel_id=1, source_target_pairs={{0,12},{4,0},{8,4},{12,8},{1,13},{5,1},{9,5},{13,9},{2,14},{6,2},{... | collective-permute-start | bytes 44072 | tf_op jit(solution)/shard_map/ppermute | solution.py:20
  47.8 1.8 %collective-permute-done.7 = f32[3,8,153]{2,1,0:T(8,128)S(1)} collective-permute-done((f32[3,8,153]{2,1,0:T(8,128)S(1)}, f32[3,8,153]{2,1,0:T(8,128)S(1)}, u32[]{:S(2)}, u32[]{:S(2)}) %collective-permute-start.7) | collective-permute-done | bytes 14720 | tf_op jit(solution)/shard_map/ppermute | solution.py:20
  49.9 1.1 collective-permute-done.8
  53.7 1.1 fusion.1
  54.8 1.1 fusion.59
  56.4 1.0 collective-permute-done.9
  57.8 5.6 %collective-permute-done.10 = f32[3,8,153]{2,1,0:T(8,128)S(1)} collective-permute-done((f32[3,8,153]{2,1,0:T(8,128)S(1)}, f32[3,8,153]{2,1,0:T(8,128)S(1)}, u32[]{:S(2)}, u32[]{:S(2)}) %collective-permute-start.10) | collective-permute-done | bytes 14720 | tf_op jit(solution)/shard_map/ppermute | solution.py:20
  63.5 1.5 collective-permute-start.11
  65.3 2.0 %collective-permute-done.11 = f32[3,8,34]{2,1,0:T(8,128)S(1)} collective-permute-done((f32[3,8,34]{2,1,0:T(8,128)S(1)}, f32[3,8,34]{2,1,0:T(8,128)S(1)}, u32[]{:S(2)}, u32[]{:S(2)}) %collective-permute-start.11) | collective-permute-done | bytes 3296 | tf_op jit(solution)/shard_map/ppermute | solution.py:20
  67.7 7.2 %scatter_fusion.1 = f32[3,8,128]{1,0,2:T(4,128)S(1)} fusion(f32[3,8,128]{1,0,2:T(4,128)S(1)} %copy.121, s32[178]{0:T(256)S(1)} %compare_select_fusion, f32[178,3,8]{2,1,0:T(4,128)S(1)} %copy.107), kind=kCustom, calls=%fused_computation.5 | custom fusion | flops 4272 | bytes 51976 | tf_op jit(solution)/shard_map/scatter-add | solution.py:143
  76.7 1.5 collective-permute-start.12
  78.3 2.1 %collective-permute-done.12 = f32[3,8,34]{2,1,0:T(8,128)S(1)} collective-permute-done((f32[3,8,34]{2,1,0:T(8,128)S(1)}, f32[3,8,34]{2,1,0:T(8,128)S(1)}, u32[]{:S(2)}, u32[]{:S(2)}) %collective-permute-start.12) | collective-permute-done | bytes 3296 | tf_op jit(solution)/shard_map/ppermute | solution.py:20
  80.6 2.0 %collective-permute-start.13 = (f32[3,8,153]{2,1,0:T(8,128)S(1)}, f32[3,8,153]{2,1,0:T(8,128)S(1)}, u32[]{:S(2)}, u32[]{:S(2)}) collective-permute-start(f32[3,8,153]{2,1,0:T(8,128)S(1)} %pad_maximum_fusion.4), channel_id=1, source_target_pairs={{0,12},{4,0},{8,4},{12,8},{1,13},{5,1},{9,5},{13,9},{2,14},{6,2},{... | collective-permute-start | bytes 44072 | tf_op jit(solution)/shard_map/ppermute | solution.py:20
  82.7 1.8 %collective-permute-done.13 = f32[3,8,153]{2,1,0:T(8,128)S(1)} collective-permute-done((f32[3,8,153]{2,1,0:T(8,128)S(1)}, f32[3,8,153]{2,1,0:T(8,128)S(1)}, u32[]{:S(2)}, u32[]{:S(2)}) %collective-permute-start.13) | collective-permute-done | bytes 14720 | tf_op jit(solution)/shard_map/ppermute | solution.py:20
  84.7 1.1 collective-permute-done.14
  88.5 1.1 fusion
  89.6 1.1 fusion.61
  91.2 1.0 collective-permute-done.15
  92.4 5.6 %collective-permute-done.16 = f32[3,8,153]{2,1,0:T(8,128)S(1)} collective-permute-done((f32[3,8,153]{2,1,0:T(8,128)S(1)}, f32[3,8,153]{2,1,0:T(8,128)S(1)}, u32[]{:S(2)}, u32[]{:S(2)}) %collective-permute-start.16) | collective-permute-done | bytes 14720 | tf_op jit(solution)/shard_map/ppermute | solution.py:20
  98.2 1.5 collective-permute-start.17
  99.9 2.0 %collective-permute-done.17 = f32[3,8,34]{2,1,0:T(8,128)S(1)} collective-permute-done((f32[3,8,34]{2,1,0:T(8,128)S(1)}, f32[3,8,34]{2,1,0:T(8,128)S(1)}, u32[]{:S(2)}, u32[]{:S(2)}) %collective-permute-start.17) | collective-permute-done | bytes 3296 | tf_op jit(solution)/shard_map/ppermute | solution.py:20
  102.4 7.2 %scatter_fusion.2 = f32[3,8,128]{1,0,2:T(4,128)S(1)} fusion(f32[3,8,128]{1,0,2:T(4,128)S(1)} %copy.122, s32[178]{0:T(256)S(1)} %compare_select_fusion, f32[178,3,8]{2,1,0:T(4,128)S(1)} %copy.112), kind=kCustom, calls=%fused_computation.6 | custom fusion | flops 4272 | bytes 51976 | tf_op jit(solution)/shard_map/scatter-add | solution.py:143
  111.9 1.5 collective-permute-start.18
  113.5 2.1 %collective-permute-done.18 = f32[3,8,34]{2,1,0:T(8,128)S(1)} collective-permute-done((f32[3,8,34]{2,1,0:T(8,128)S(1)}, f32[3,8,34]{2,1,0:T(8,128)S(1)}, u32[]{:S(2)}, u32[]{:S(2)}) %collective-permute-start.18) | collective-permute-done | bytes 3296 | tf_op jit(solution)/shard_map/ppermute | solution.py:20
  115.9 2.2 %collective-permute-start.19 = (f32[3,8,153]{2,1,0:T(8,128)S(1)}, f32[3,8,153]{2,1,0:T(8,128)S(1)}, u32[]{:S(2)}, u32[]{:S(2)}) collective-permute-start(f32[3,8,153]{2,1,0:T(8,128)S(1)} %pad_maximum_fusion.6), channel_id=1, source_target_pairs={{0,12},{4,0},{8,4},{12,8},{1,13},{5,1},{9,5},{13,9},{2,14},{6,2},{... | collective-permute-start | bytes 44072 | tf_op jit(solution)/shard_map/ppermute | solution.py:20
  118.1 1.8 %collective-permute-done.19 = f32[3,8,153]{2,1,0:T(8,128)S(1)} collective-permute-done((f32[3,8,153]{2,1,0:T(8,128)S(1)}, f32[3,8,153]{2,1,0:T(8,128)S(1)}, u32[]{:S(2)}, u32[]{:S(2)}) %collective-permute-start.19) | collective-permute-done | bytes 14720 | tf_op jit(solution)/shard_map/ppermute | solution.py:20
  120.2 1.1 collective-permute-done.20
  123.3 1.1 fusion.66
  124.9 1.1 fusion.2
  125.9 1.1 fusion.57
  131.3 3.1 %collective-permute-done.22 = f32[3,8,153]{2,1,0:T(8,128)S(1)} collective-permute-done((f32[3,8,153]{2,1,0:T(8,128)S(1)}, f32[3,8,153]{2,1,0:T(8,128)S(1)}, u32[]{:S(2)}, u32[]{:S(2)}) %collective-permute-start.22) | collective-permute-done | bytes 14720 | tf_op jit(solution)/shard_map/ppermute | solution.py:20
  134.5 1.5 collective-permute-start.23
  137.0 1.2 collective-permute-done.23
  138.7 7.2 %scatter_fusion.3 = f32[3,8,128]{1,0,2:T(4,128)S(1)} fusion(f32[3,8,128]{1,0,2:T(4,128)S(1)} %copy.123, s32[178]{0:T(256)S(1)} %compare_select_fusion, f32[178,3,8]{2,1,0:T(4,128)S(1)} %copy.117), kind=kCustom, calls=%fused_computation.7 | custom fusion | flops 4272 | bytes 51976 | tf_op jit(solution)/shard_map/scatter-add | solution.py:143
  146.0 1.2 multiply_reduce_fusion
  147.9 29.9 %psum.7 = f32[3,2]{1,0:T(4,128)S(1)} all-reduce(f32[3,2]{1,0:T(4,128)S(1)} %pad_maximum_fusion.24), channel_id=1, replica_groups=mesh['runs'=2,'gx'=4,'gy'=2,'gz'=2] {'gx','gy','gz'}, use_global_device_ids=true, to_apply=%region_34.36 | all-reduce | flops 6 | bytes 48 | tf_op jit(solution)/shard_map/psum | solution.py:220
  (278 shorter events, 32.6 us)
Async XLA Ops:
  2.0 5.2 %copy-start.4 = (s32[2,1792]{1,0:T(2,128)S(1)}, s32[2,1792]{1,0:T(2,128)}, u32[]{:S(2)}) copy-start(s32[2,1792]{1,0:T(2,128)} %param.14) | copy-start | bytes 43012
  3.9 12.3 %copy-start.3 = (f32[3,178]{1,0:T(4,128)S(1)}, f32[3,178]{1,0:T(4,128)}, u32[]{:S(2)}) copy-start(f32[3,178]{1,0:T(4,128)} %constant.57.clone) | copy-start | bytes 6412
  3.9 12.3 %copy-start = (f32[3,8,128]{2,1,0:T(8,128)S(1)}, f32[3,8,128]{2,1,0:T(8,128)}, u32[]{:S(2)}) copy-start(f32[3,8,128]{2,1,0:T(8,128)} %param.11) | copy-start | bytes 36868
  4.1 4.6 %collective-permute-start = (f32[3,8,34]{2,1,0:T(8,128)S(1)}, f32[3,8,34]{2,1,0:T(8,128)S(1)}, u32[]{:S(2)}, u32[]{:S(2)}) collective-permute-start(f32[3,8,34]{2,1,0:T(8,128)S(1)} %pad_maximum_fusion.8), channel_id=1, source_target_pairs={{0,2},{2,0},{1,3},{3,1},{4,6},{6,4},{5,7},{7,5},{8,10},{10,8},{9,1... | collective-permute-start | bytes 9800 | tf_op jit(solution)/shard_map/ppermute | solution.py:20
  9.0 5.7 %collective-permute-start.1 = (f32[3,8,153]{2,1,0:T(8,128)S(1)}, f32[3,8,153]{2,1,0:T(8,128)S(1)}, u32[]{:S(2)}, u32[]{:S(2)}) collective-permute-start(f32[3,8,153]{2,1,0:T(8,128)S(1)} %pad_maximum_fusion), channel_id=1, source_target_pairs={{0,12},{4,0},{8,4},{12,8},{1,13},{5,1},{9,5},{13,9},{2,14},{6,2},{... | collective-permute-start | bytes 44072 | tf_op jit(solution)/shard_map/ppermute | solution.py:20
  14.8 1.2 collective-permute-start.2
  19.8 10.4 %copy-start.1 = (s32[7,128]{1,0:T(8,128)S(1)}, s32[7,128]{1,0:T(8,128)}, u32[]{:S(2)}) copy-start(s32[7,128]{1,0:T(8,128)} %param.15) | copy-start | bytes 10756
  21.2 1.2 collective-permute-start.3
  22.7 5.9 %collective-permute-start.4 = (f32[3,8,153]{2,1,0:T(8,128)S(1)}, f32[3,8,153]{2,1,0:T(8,128)S(1)}, u32[]{:S(2)}, u32[]{:S(2)}) collective-permute-start(f32[3,8,153]{2,1,0:T(8,128)S(1)} %pad_maximum_fusion.1), channel_id=1, source_target_pairs={{0,4},{4,8},{8,12},{12,0},{1,5},{5,9},{9,13},{13,1},{2,6},{6,10},{... | collective-permute-start | bytes 44072 | tf_op jit(solution)/shard_map/ppermute | solution.py:20
  28.7 3.7 %collective-permute-start.5 = (f32[3,8,34]{2,1,0:T(8,128)S(1)}, f32[3,8,34]{2,1,0:T(8,128)S(1)}, u32[]{:S(2)}, u32[]{:S(2)}) collective-permute-start(f32[3,8,34]{2,1,0:T(8,128)S(1)} %pad_maximum_fusion.11), channel_id=1, source_target_pairs={{0,2},{2,0},{1,3},{3,1},{4,6},{6,4},{5,7},{7,5},{8,10},{10,8},{9,1... | collective-permute-start | bytes 9800 | tf_op jit(solution)/shard_map/ppermute | solution.py:20
  30.5 9.7 %copy-start.5 = (f32[3,8,128]{2,1,0:T(8,128)S(1)}, f32[3,8,128]{2,1,0:T(8,128)}, u32[]{:S(2)}) copy-start(f32[3,8,128]{2,1,0:T(8,128)} %param.12) | copy-start | bytes 36868
  41.9 3.7 %collective-permute-start.6 = (f32[3,8,34]{2,1,0:T(8,128)S(1)}, f32[3,8,34]{2,1,0:T(8,128)S(1)}, u32[]{:S(2)}, u32[]{:S(2)}) collective-permute-start(f32[3,8,34]{2,1,0:T(8,128)S(1)} %pad_maximum_fusion.12), channel_id=1, source_target_pairs={{0,2},{2,0},{1,3},{3,1},{4,6},{6,4},{5,7},{7,5},{8,10},{10,8},{9,1... | collective-permute-start | bytes 9800 | tf_op jit(solution)/shard_map/ppermute | solution.py:20
  45.8 3.8 %collective-permute-start.7 = (f32[3,8,153]{2,1,0:T(8,128)S(1)}, f32[3,8,153]{2,1,0:T(8,128)S(1)}, u32[]{:S(2)}, u32[]{:S(2)}) collective-permute-start(f32[3,8,153]{2,1,0:T(8,128)S(1)} %pad_maximum_fusion.2), channel_id=1, source_target_pairs={{0,12},{4,0},{8,4},{12,8},{1,13},{5,1},{9,5},{13,9},{2,14},{6,2},{... | collective-permute-start | bytes 44072 | tf_op jit(solution)/shard_map/ppermute | solution.py:20
  49.8 1.2 collective-permute-start.8
  56.2 1.2 collective-permute-start.9
  57.6 5.8 %collective-permute-start.10 = (f32[3,8,153]{2,1,0:T(8,128)S(1)}, f32[3,8,153]{2,1,0:T(8,128)S(1)}, u32[]{:S(2)}, u32[]{:S(2)}) collective-permute-start(f32[3,8,153]{2,1,0:T(8,128)S(1)} %pad_maximum_fusion.3), channel_id=1, source_target_pairs={{0,4},{4,8},{8,12},{12,0},{1,5},{5,9},{9,13},{13,1},{2,6},{6,10},{... | collective-permute-start | bytes 44072 | tf_op jit(solution)/shard_map/ppermute | solution.py:20
  63.5 3.7 %collective-permute-start.11 = (f32[3,8,34]{2,1,0:T(8,128)S(1)}, f32[3,8,34]{2,1,0:T(8,128)S(1)}, u32[]{:S(2)}, u32[]{:S(2)}) collective-permute-start(f32[3,8,34]{2,1,0:T(8,128)S(1)} %pad_maximum_fusion.15), channel_id=1, source_target_pairs={{0,2},{2,0},{1,3},{3,1},{4,6},{6,4},{5,7},{7,5},{8,10},{10,8},{9,1... | collective-permute-start | bytes 9800 | tf_op jit(solution)/shard_map/ppermute | solution.py:20
  76.7 3.7 %collective-permute-start.12 = (f32[3,8,34]{2,1,0:T(8,128)S(1)}, f32[3,8,34]{2,1,0:T(8,128)S(1)}, u32[]{:S(2)}, u32[]{:S(2)}) collective-permute-start(f32[3,8,34]{2,1,0:T(8,128)S(1)} %pad_maximum_fusion.16), channel_id=1, source_target_pairs={{0,2},{2,0},{1,3},{3,1},{4,6},{6,4},{5,7},{7,5},{8,10},{10,8},{9,1... | collective-permute-start | bytes 9800 | tf_op jit(solution)/shard_map/ppermute | solution.py:20
  80.6 3.8 %collective-permute-start.13 = (f32[3,8,153]{2,1,0:T(8,128)S(1)}, f32[3,8,153]{2,1,0:T(8,128)S(1)}, u32[]{:S(2)}, u32[]{:S(2)}) collective-permute-start(f32[3,8,153]{2,1,0:T(8,128)S(1)} %pad_maximum_fusion.4), channel_id=1, source_target_pairs={{0,12},{4,0},{8,4},{12,8},{1,13},{5,1},{9,5},{13,9},{2,14},{6,2},{... | collective-permute-start | bytes 44072 | tf_op jit(solution)/shard_map/ppermute | solution.py:20
  84.6 1.2 collective-permute-start.14
  91.0 1.2 collective-permute-start.15
  92.4 5.6 %collective-permute-start.16 = (f32[3,8,153]{2,1,0:T(8,128)S(1)}, f32[3,8,153]{2,1,0:T(8,128)S(1)}, u32[]{:S(2)}, u32[]{:S(2)}) collective-permute-start(f32[3,8,153]{2,1,0:T(8,128)S(1)} %pad_maximum_fusion.5), channel_id=1, source_target_pairs={{0,4},{4,8},{8,12},{12,0},{1,5},{5,9},{9,13},{13,1},{2,6},{6,10},{... | collective-permute-start | bytes 44072 | tf_op jit(solution)/shard_map/ppermute | solution.py:20
  98.2 3.7 %collective-permute-start.17 = (f32[3,8,34]{2,1,0:T(8,128)S(1)}, f32[3,8,34]{2,1,0:T(8,128)S(1)}, u32[]{:S(2)}, u32[]{:S(2)}) collective-permute-start(f32[3,8,34]{2,1,0:T(8,128)S(1)} %pad_maximum_fusion.19), channel_id=1, source_target_pairs={{0,2},{2,0},{1,3},{3,1},{4,6},{6,4},{5,7},{7,5},{8,10},{10,8},{9,1... | collective-permute-start | bytes 9800 | tf_op jit(solution)/shard_map/ppermute | solution.py:20
  110.5 35.4 %copy-start.2 = (f32[3,8,128]{2,1,0:T(8,128)}, f32[3,8,128]{2,1,0:T(8,128)S(1)}, u32[]{:S(2)}) copy-start(f32[3,8,128]{2,1,0:T(8,128)S(1)} %pad_add_fusion) | copy-start | bytes 36868
  111.9 3.7 %collective-permute-start.18 = (f32[3,8,34]{2,1,0:T(8,128)S(1)}, f32[3,8,34]{2,1,0:T(8,128)S(1)}, u32[]{:S(2)}, u32[]{:S(2)}) collective-permute-start(f32[3,8,34]{2,1,0:T(8,128)S(1)} %pad_maximum_fusion.20), channel_id=1, source_target_pairs={{0,2},{2,0},{1,3},{3,1},{4,6},{6,4},{5,7},{7,5},{8,10},{10,8},{9,1... | collective-permute-start | bytes 9800 | tf_op jit(solution)/shard_map/ppermute | solution.py:20
  115.9 4.0 %collective-permute-start.19 = (f32[3,8,153]{2,1,0:T(8,128)S(1)}, f32[3,8,153]{2,1,0:T(8,128)S(1)}, u32[]{:S(2)}, u32[]{:S(2)}) collective-permute-start(f32[3,8,153]{2,1,0:T(8,128)S(1)} %pad_maximum_fusion.6), channel_id=1, source_target_pairs={{0,12},{4,0},{8,4},{12,8},{1,13},{5,1},{9,5},{13,9},{2,14},{6,2},{... | collective-permute-start | bytes 44072 | tf_op jit(solution)/shard_map/ppermute | solution.py:20
  120.1 1.2 collective-permute-start.20
  127.3 1.2 collective-permute-start.21
  128.8 5.6 %collective-permute-start.22 = (f32[3,8,153]{2,1,0:T(8,128)S(1)}, f32[3,8,153]{2,1,0:T(8,128)S(1)}, u32[]{:S(2)}, u32[]{:S(2)}) collective-permute-start(f32[3,8,153]{2,1,0:T(8,128)S(1)} %pad_maximum_fusion.7), channel_id=1, source_target_pairs={{0,4},{4,8},{8,12},{12,0},{1,5},{5,9},{9,13},{13,1},{2,6},{6,10},{... | collective-permute-start | bytes 44072 | tf_op jit(solution)/shard_map/ppermute | solution.py:20
  134.5 3.7 %collective-permute-start.23 = (f32[3,8,34]{2,1,0:T(8,128)S(1)}, f32[3,8,34]{2,1,0:T(8,128)S(1)}, u32[]{:S(2)}, u32[]{:S(2)}) collective-permute-start(f32[3,8,34]{2,1,0:T(8,128)S(1)} %pad_maximum_fusion.23), channel_id=1, source_target_pairs={{0,2},{2,0},{1,3},{3,1},{4,6},{6,4},{5,7},{7,5},{8,10},{10,8},{9,1... | collective-permute-start | bytes 9800 | tf_op jit(solution)/shard_map/ppermute | solution.py:20
where the time goes:
time: 179 us
  waiting for transfers between devices  50.2 us (28%)
  other arithmetic  38.8 us (22%)
  blocking collectives  29.9 us (17%)
  starting transfers between devices  25.1 us (14%)
  matrix products  15.5 us (9%)
  local copies, waits for them, and re-layouts  13.6 us (8%)
  between operations  5.39 us (3%)
    ppermute x24, waiting for transfers between devices, from_behind(): lax.ppermute(value, axis, [(i, (i + by) % count) for i in range(count)])  50.2 us
    psum x1, blocking collectives, on_device(): energies = lax.psum(energies, ('gx', 'gy', 'gz'))  29.9 us
    scatter-add x4, other arithmetic, local_forces(): home_forces = forces[:, :, :cluster_count].at[:, :, send_list].add(returned)  28.6 us
    ppermute x24, starting transfers between devices, from_behind(): lax.ppermute(value, axis, [(i, (i + by) % count) for i in range(count)])  25.1 us
    slice x92, local copies, waits for them, and re-layouts, split_blocks(): pieces.append(packed[:, :, position:position + length])  4.99 us
    dot_general x4, matrix products, domain_forces(): lax.dot_general(on_first, tables[0], contract, precision=lax.Precision.HI...  4.36 us
    dot_general x4, matrix products, domain_forces(): lax.dot_general(on_second, tables[1], contract, precision=lax.Precision.H...  4.27 us
    gather x8, local copies, waits for them, and re-layouts, share_coords(): outgoing = split_blocks(jnp.take(coords, send_list, axis=2), sizes_all)  3.98 us
  transfers between devices with their start and end apart: 24, of which 24 were waited for; matrix products, arithmetic and copies ran while one was open for 1% of the time, Pallas kernels for 0%

commit v1 on v0

--- a/solution.py
+++ b/solution.py
@@ -217,7 +217,8 @@
         kinetic = 0.5 * jnp.sum(velocities * velocities)
         energy_rows.append(jnp.stack([potential, kinetic]))
     energies = jnp.stack(energy_rows)
-    energies = lax.psum(energies, ("gx", "gy", "gz"))
+    shards = lax.all_gather(energies, ("gx", "gy", "gz"), axis=0, tiled=False)
+    energies = shards.sum(axis=0)
     return (positions, velocities, energies / bead_total)
 
 

time: 179 us -> 169 us (0.944)
  blocking collectives: 29.9 us -> 20 us
    psum x1 -> x0, blocking collectives: 29.9 us -> none  [on_device(): energies = lax.psum(energies, ('gx', 'gy', 'gz'))]
    all_gather x0 -> x1, blocking collectives: none -> 20 us  [on_device(): shards = lax.all_gather(energies, ('gx', 'gy', 'gz'), axis=0, tiled=False)]
where the time goes in v1:
time: 169 us
  waiting for transfers between devices  50.2 us (30%)
  other arithmetic  39.4 us (23%)
  starting transfers between devices  25.1 us (15%)
  blocking collectives  20 us (12%)
  matrix products  15.5 us (9%)
  local copies, waits for them, and re-layouts  13 us (8%)
  between operations  5.39 us (3%)
    ppermute x24, waiting for transfers between devices, from_behind(): lax.ppermute(value, axis, [(i, (i + by) % count) for i in range(count)])  50.2 us
    scatter-add x4, other arithmetic, local_forces(): home_forces = forces[:, :, :cluster_count].at[:, :, send_list].add(returned)  28.6 us
    ppermute x24, starting transfers between devices, from_behind(): lax.ppermute(value, axis, [(i, (i + by) % count) for i in range(count)])  25.1 us
    all_gather x1, blocking collectives, on_device(): shards = lax.all_gather(energies, ('gx', 'gy', 'gz'), axis=0, tiled=False)  20 us
    slice x92, local copies, waits for them, and re-layouts, split_blocks(): pieces.append(packed[:, :, position:position + length])  4.99 us
    dot_general x4, matrix products, domain_forces(): lax.dot_general(on_first, tables[0], contract, precision=lax.Precision.HI...  4.36 us
    dot_general x4, matrix products, domain_forces(): lax.dot_general(on_second, tables[1], contract, precision=lax.Precision.H...  4.27 us
    gather x8, local copies, waits for them, and re-layouts, share_coords(): outgoing = split_blocks(jnp.take(coords, send_list, axis=2), sizes_all)  3.98 us
  transfers between devices with their start and end apart: 24, of which 24 were waited for; matrix products, arithmetic and copies ran while one was open for 1% of the time, Pallas kernels for 0%

profile of v1, /device:TPU:0, one launch (start us, length us, event | category | flops | bytes accessed | tf_op | source)
XLA Modules:
  0.0 168.7 jit_solution(3047174580836648677)
XLA Ops:
  4.1 3.0 %collective-permute-start = (f32[3,8,34]{2,1,0:T(8,128)S(1)}, f32[3,8,34]{2,1,0:T(8,128)S(1)}, u32[]{:S(2)}, u32[]{:S(2)}) collective-permute-start(f32[3,8,34]{2,1,0:T(8,128)S(1)} %pad_maximum_fusion.8), channel_id=1, source_target_pairs={{0,2},{2,0},{1,3},{3,1},{4,6},{6,4},{5,7},{7,5},{8,10},{10,8},{9,1... | collective-permute-start | bytes 9800 | tf_op jit(solution)/shard_map/ppermute | solution.py:20
  7.2 1.5 collective-permute-done
  9.0 4.1 %collective-permute-start.1 = (f32[3,8,153]{2,1,0:T(8,128)S(1)}, f32[3,8,153]{2,1,0:T(8,128)S(1)}, u32[]{:S(2)}, u32[]{:S(2)}) collective-permute-start(f32[3,8,153]{2,1,0:T(8,128)S(1)} %pad_maximum_fusion), channel_id=1, source_target_pairs={{0,12},{4,0},{8,4},{12,8},{1,13},{5,1},{9,5},{13,9},{2,14},{6,2},{... | collective-permute-start | bytes 44072 | tf_op jit(solution)/shard_map/ppermute | solution.py:20
  13.2 1.5 collective-permute-done.1
  18.8 1.1 fusion.3
  19.9 1.1 fusion.55
  21.4 1.0 collective-permute-done.3
  22.9 5.6 %collective-permute-done.4 = f32[3,8,153]{2,1,0:T(8,128)S(1)} collective-permute-done((f32[3,8,153]{2,1,0:T(8,128)S(1)}, f32[3,8,153]{2,1,0:T(8,128)S(1)}, u32[]{:S(2)}, u32[]{:S(2)}) %collective-permute-start.4) | collective-permute-done | bytes 14720 | tf_op jit(solution)/shard_map/ppermute | solution.py:20
  28.7 1.5 collective-permute-start.5
  30.5 2.0 %collective-permute-done.5 = f32[3,8,34]{2,1,0:T(8,128)S(1)} collective-permute-done((f32[3,8,34]{2,1,0:T(8,128)S(1)}, f32[3,8,34]{2,1,0:T(8,128)S(1)}, u32[]{:S(2)}, u32[]{:S(2)}) %collective-permute-start.5) | collective-permute-done | bytes 3296 | tf_op jit(solution)/shard_map/ppermute | solution.py:20
  32.9 7.2 %scatter_fusion = f32[3,8,128]{1,0,2:T(4,128)S(1)} fusion(f32[3,8,128]{1,0,2:T(4,128)S(1)} %copy.120, s32[178]{0:T(256)S(1)} %compare_select_fusion, f32[178,3,8]{2,1,0:T(4,128)S(1)} %copy.102), kind=kCustom, calls=%fused_computation.4 | custom fusion | flops 4272 | bytes 51976 | tf_op jit(solution)/shard_map/scatter-add | solution.py:143
  41.9 1.5 collective-permute-start.6
  43.4 2.1 %collective-permute-done.6 = f32[3,8,34]{2,1,0:T(8,128)S(1)} collective-permute-done((f32[3,8,34]{2,1,0:T(8,128)S(1)}, f32[3,8,34]{2,1,0:T(8,128)S(1)}, u32[]{:S(2)}, u32[]{:S(2)}) %collective-permute-start.6) | collective-permute-done | bytes 3296 | tf_op jit(solution)/shard_map/ppermute | solution.py:20
  45.8 2.0 %collective-permute-start.7 = (f32[3,8,153]{2,1,0:T(8,128)S(1)}, f32[3,8,153]{2,1,0:T(8,128)S(1)}, u32[]{:S(2)}, u32[]{:S(2)}) collective-permute-start(f32[3,8,153]{2,1,0:T(8,128)S(1)} %pad_maximum_fusion.2), channel_id=1, source_target_pairs={{0,12},{4,0},{8,4},{12,8},{1,13},{5,1},{9,5},{13,9},{2,14},{6,2},{... | collective-permute-start | bytes 44072 | tf_op jit(solution)/shard_map/ppermute | solution.py:20
  47.8 1.8 %collective-permute-done.7 = f32[3,8,153]{2,1,0:T(8,128)S(1)} collective-permute-done((f32[3,8,153]{2,1,0:T(8,128)S(1)}, f32[3,8,153]{2,1,0:T(8,128)S(1)}, u32[]{:S(2)}, u32[]{:S(2)}) %collective-permute-start.7) | collective-permute-done | bytes 14720 | tf_op jit(solution)/shard_map/ppermute | solution.py:20
  49.9 1.1 collective-permute-done.8
  53.7 1.1 fusion.1
  54.8 1.1 fusion.59
  56.4 1.0 collective-permute-done.9
  57.8 5.6 %collective-permute-done.10 = f32[3,8,153]{2,1,0:T(8,128)S(1)} collective-permute-done((f32[3,8,153]{2,1,0:T(8,128)S(1)}, f32[3,8,153]{2,1,0:T(8,128)S(1)}, u32[]{:S(2)}, u32[]{:S(2)}) %collective-permute-start.10) | collective-permute-done | bytes 14720 | tf_op jit(solution)/shard_map/ppermute | solution.py:20
  63.5 1.5 collective-permute-start.11
  65.3 2.0 %collective-permute-done.11 = f32[3,8,34]{2,1,0:T(8,128)S(1)} collective-permute-done((f32[3,8,34]{2,1,0:T(8,128)S(1)}, f32[3,8,34]{2,1,0:T(8,128)S(1)}, u32[]{:S(2)}, u32[]{:S(2)}) %collective-permute-start.11) | collective-permute-done | bytes 3296 | tf_op jit(solution)/shard_map/ppermute | solution.py:20
  67.7 7.2 %scatter_fusion.1 = f32[3,8,128]{1,0,2:T(4,128)S(1)} fusion(f32[3,8,128]{1,0,2:T(4,128)S(1)} %copy.121, s32[178]{0:T(256)S(1)} %compare_select_fusion, f32[178,3,8]{2,1,0:T(4,128)S(1)} %copy.107), kind=kCustom, calls=%fused_computation.5 | custom fusion | flops 4272 | bytes 51976 | tf_op jit(solution)/shard_map/scatter-add | solution.py:143
  76.7 1.5 collective-permute-start.12
  78.3 2.1 %collective-permute-done.12 = f32[3,8,34]{2,1,0:T(8,128)S(1)} collective-permute-done((f32[3,8,34]{2,1,0:T(8,128)S(1)}, f32[3,8,34]{2,1,0:T(8,128)S(1)}, u32[]{:S(2)}, u32[]{:S(2)}) %collective-permute-start.12) | collective-permute-done | bytes 3296 | tf_op jit(solution)/shard_map/ppermute | solution.py:20
  80.6 2.0 %collective-permute-start.13 = (f32[3,8,153]{2,1,0:T(8,128)S(1)}, f32[3,8,153]{2,1,0:T(8,128)S(1)}, u32[]{:S(2)}, u32[]{:S(2)}) collective-permute-start(f32[3,8,153]{2,1,0:T(8,128)S(1)} %pad_maximum_fusion.4), channel_id=1, source_target_pairs={{0,12},{4,0},{8,4},{12,8},{1,13},{5,1},{9,5},{13,9},{2,14},{6,2},{... | collective-permute-start | bytes 44072 | tf_op jit(solution)/shard_map/ppermute | solution.py:20
  82.7 1.8 %collective-permute-done.13 = f32[3,8,153]{2,1,0:T(8,128)S(1)} collective-permute-done((f32[3,8,153]{2,1,0:T(8,128)S(1)}, f32[3,8,153]{2,1,0:T(8,128)S(1)}, u32[]{:S(2)}, u32[]{:S(2)}) %collective-permute-start.13) | collective-permute-done | bytes 14720 | tf_op jit(solution)/shard_map/ppermute | solution.py:20
  84.7 1.1 collective-permute-done.14
  88.5 1.1 fusion
  89.6 1.1 fusion.61
  92.4 5.6 %collective-permute-done.16 = f32[3,8,153]{2,1,0:T(8,128)S(1)} collective-permute-done((f32[3,8,153]{2,1,0:T(8,128)S(1)}, f32[3,8,153]{2,1,0:T(8,128)S(1)}, u32[]{:S(2)}, u32[]{:S(2)}) %collective-permute-start.16) | collective-permute-done | bytes 14720 | tf_op jit(solution)/shard_map/ppermute | solution.py:20
  98.2 1.5 collective-permute-start.17
  99.9 2.0 %collective-permute-done.17 = f32[3,8,34]{2,1,0:T(8,128)S(1)} collective-permute-done((f32[3,8,34]{2,1,0:T(8,128)S(1)}, f32[3,8,34]{2,1,0:T(8,128)S(1)}, u32[]{:S(2)}, u32[]{:S(2)}) %collective-permute-start.17) | collective-permute-done | bytes 3296 | tf_op jit(solution)/shard_map/ppermute | solution.py:20
  102.4 7.2 %scatter_fusion.2 = f32[3,8,128]{1,0,2:T(4,128)S(1)} fusion(f32[3,8,128]{1,0,2:T(4,128)S(1)} %copy.122, s32[178]{0:T(256)S(1)} %compare_select_fusion, f32[178,3,8]{2,1,0:T(4,128)S(1)} %copy.112), kind=kCustom, calls=%fused_computation.6 | custom fusion | flops 4272 | bytes 51976 | tf_op jit(solution)/shard_map/scatter-add | solution.py:143
  111.9 1.5 collective-permute-start.18
  113.5 2.1 %collective-permute-done.18 = f32[3,8,34]{2,1,0:T(8,128)S(1)} collective-permute-done((f32[3,8,34]{2,1,0:T(8,128)S(1)}, f32[3,8,34]{2,1,0:T(8,128)S(1)}, u32[]{:S(2)}, u32[]{:S(2)}) %collective-permute-start.18) | collective-permute-done | bytes 3296 | tf_op jit(solution)/shard_map/ppermute | solution.py:20
  115.9 2.2 %collective-permute-start.19 = (f32[3,8,153]{2,1,0:T(8,128)S(1)}, f32[3,8,153]{2,1,0:T(8,128)S(1)}, u32[]{:S(2)}, u32[]{:S(2)}) collective-permute-start(f32[3,8,153]{2,1,0:T(8,128)S(1)} %pad_maximum_fusion.6), channel_id=1, source_target_pairs={{0,12},{4,0},{8,4},{12,8},{1,13},{5,1},{9,5},{13,9},{2,14},{6,2},{... | collective-permute-start | bytes 44072 | tf_op jit(solution)/shard_map/ppermute | solution.py:20
  118.1 1.8 %collective-permute-done.19 = f32[3,8,153]{2,1,0:T(8,128)S(1)} collective-permute-done((f32[3,8,153]{2,1,0:T(8,128)S(1)}, f32[3,8,153]{2,1,0:T(8,128)S(1)}, u32[]{:S(2)}, u32[]{:S(2)}) %collective-permute-start.19) | collective-permute-done | bytes 14720 | tf_op jit(solution)/shard_map/ppermute | solution.py:20
  120.2 1.1 collective-permute-done.20
  123.3 1.1 fusion.66
  124.9 1.1 fusion.2
  125.9 1.1 fusion.57
  131.3 3.1 %collective-permute-done.22 = f32[3,8,153]{2,1,0:T(8,128)S(1)} collective-permute-done((f32[3,8,153]{2,1,0:T(8,128)S(1)}, f32[3,8,153]{2,1,0:T(8,128)S(1)}, u32[]{:S(2)}, u32[]{:S(2)}) %collective-permute-start.22) | collective-permute-done | bytes 14720 | tf_op jit(solution)/shard_map/ppermute | solution.py:20
  134.5 1.5 collective-permute-start.23
  137.0 1.2 collective-permute-done.23
  138.7 7.2 %scatter_fusion.3 = f32[3,8,128]{1,0,2:T(4,128)S(1)} fusion(f32[3,8,128]{1,0,2:T(4,128)S(1)} %copy.123, s32[178]{0:T(256)S(1)} %compare_select_fusion, f32[178,3,8]{2,1,0:T(4,128)S(1)} %copy.117), kind=kCustom, calls=%fused_computation.7 | custom fusion | flops 4272 | bytes 51976 | tf_op jit(solution)/shard_map/scatter-add | solution.py:143
  146.0 1.2 multiply_reduce_fusion
  148.0 20.0 %all-gather.1 = f32[16,3,2]{1,2,0:T(2,128)S(1)} all-gather(f32[1,3,2]{1,2,0:T(2,128)S(1)} %bitcast.82), channel_id=2, replica_groups=mesh['runs'=2,'gx'=4,'gy'=2,'gz'=2] {'gx','gy','gz'}, dimensions={0}, use_global_device_ids=true | all-gather | bytes 408 | tf_op jit(solution)/shard_map/all_gather | solution.py:220
  (279 shorter events, 32.6 us)
Async XLA Ops:
  2.0 5.2 %copy-start.4 = (s32[2,1792]{1,0:T(2,128)S(1)}, s32[2,1792]{1,0:T(2,128)}, u32[]{:S(2)}) copy-start(s32[2,1792]{1,0:T(2,128)} %param.14) | copy-start | bytes 43012
  3.9 12.3 %copy-start.3 = (f32[3,178]{1,0:T(4,128)S(1)}, f32[3,178]{1,0:T(4,128)}, u32[]{:S(2)}) copy-start(f32[3,178]{1,0:T(4,128)} %constant.57.clone) | copy-start | bytes 6412
  3.9 12.3 %copy-start = (f32[3,8,128]{2,1,0:T(8,128)S(1)}, f32[3,8,128]{2,1,0:T(8,128)}, u32[]{:S(2)}) copy-start(f32[3,8,128]{2,1,0:T(8,128)} %param.11) | copy-start | bytes 36868
  4.1 4.6 %collective-permute-start = (f32[3,8,34]{2,1,0:T(8,128)S(1)}, f32[3,8,34]{2,1,0:T(8,128)S(1)}, u32[]{:S(2)}, u32[]{:S(2)}) collective-permute-start(f32[3,8,34]{2,1,0:T(8,128)S(1)} %pad_maximum_fusion.8), channel_id=1, source_target_pairs={{0,2},{2,0},{1,3},{3,1},{4,6},{6,4},{5,7},{7,5},{8,10},{10,8},{9,1... | collective-permute-start | bytes 9800 | tf_op jit(solution)/shard_map/ppermute | solution.py:20
  9.0 5.7 %collective-permute-start.1 = (f32[3,8,153]{2,1,0:T(8,128)S(1)}, f32[3,8,153]{2,1,0:T(8,128)S(1)}, u32[]{:S(2)}, u32[]{:S(2)}) collective-permute-start(f32[3,8,153]{2,1,0:T(8,128)S(1)} %pad_maximum_fusion), channel_id=1, source_target_pairs={{0,12},{4,0},{8,4},{12,8},{1,13},{5,1},{9,5},{13,9},{2,14},{6,2},{... | collective-permute-start | bytes 44072 | tf_op jit(solution)/shard_map/ppermute | solution.py:20
  14.8 1.2 collective-permute-start.2
  19.8 10.4 %copy-start.1 = (s32[7,128]{1,0:T(8,128)S(1)}, s32[7,128]{1,0:T(8,128)}, u32[]{:S(2)}) copy-start(s32[7,128]{1,0:T(8,128)} %param.15) | copy-start | bytes 10756
  21.2 1.2 collective-permute-start.3
  22.7 5.9 %collective-permute-start.4 = (f32[3,8,153]{2,1,0:T(8,128)S(1)}, f32[3,8,153]{2,1,0:T(8,128)S(1)}, u32[]{:S(2)}, u32[]{:S(2)}) collective-permute-start(f32[3,8,153]{2,1,0:T(8,128)S(1)} %pad_maximum_fusion.1), channel_id=1, source_target_pairs={{0,4},{4,8},{8,12},{12,0},{1,5},{5,9},{9,13},{13,1},{2,6},{6,10},{... | collective-permute-start | bytes 44072 | tf_op jit(solution)/shard_map/ppermute | solution.py:20
  28.7 3.7 %collective-permute-start.5 = (f32[3,8,34]{2,1,0:T(8,128)S(1)}, f32[3,8,34]{2,1,0:T(8,128)S(1)}, u32[]{:S(2)}, u32[]{:S(2)}) collective-permute-start(f32[3,8,34]{2,1,0:T(8,128)S(1)} %pad_maximum_fusion.11), channel_id=1, source_target_pairs={{0,2},{2,0},{1,3},{3,1},{4,6},{6,4},{5,7},{7,5},{8,10},{10,8},{9,1... | collective-permute-start | bytes 9800 | tf_op jit(solution)/shard_map/ppermute | solution.py:20
  30.5 9.7 %copy-start.5 = (f32[3,8,128]{2,1,0:T(8,128)S(1)}, f32[3,8,128]{2,1,0:T(8,128)}, u32[]{:S(2)}) copy-start(f32[3,8,128]{2,1,0:T(8,128)} %param.12) | copy-start | bytes 36868
  41.9 3.7 %collective-permute-start.6 = (f32[3,8,34]{2,1,0:T(8,128)S(1)}, f32[3,8,34]{2,1,0:T(8,128)S(1)}, u32[]{:S(2)}, u32[]{:S(2)}) collective-permute-start(f32[3,8,34]{2,1,0:T(8,128)S(1)} %pad_maximum_fusion.12), channel_id=1, source_target_pairs={{0,2},{2,0},{1,3},{3,1},{4,6},{6,4},{5,7},{7,5},{8,10},{10,8},{9,1... | collective-permute-start | bytes 9800 | tf_op jit(solution)/shard_map/ppermute | solution.py:20
  45.8 3.8 %collective-permute-start.7 = (f32[3,8,153]{2,1,0:T(8,128)S(1)}, f32[3,8,153]{2,1,0:T(8,128)S(1)}, u32[]{:S(2)}, u32[]{:S(2)}) collective-permute-start(f32[3,8,153]{2,1,0:T(8,128)S(1)} %pad_maximum_fusion.2), channel_id=1, source_target_pairs={{0,12},{4,0},{8,4},{12,8},{1,13},{5,1},{9,5},{13,9},{2,14},{6,2},{... | collective-permute-start | bytes 44072 | tf_op jit(solution)/shard_map/ppermute | solution.py:20
  49.8 1.2 collective-permute-start.8
  56.2 1.2 collective-permute-start.9
  57.6 5.8 %collective-permute-start.10 = (f32[3,8,153]{2,1,0:T(8,128)S(1)}, f32[3,8,153]{2,1,0:T(8,128)S(1)}, u32[]{:S(2)}, u32[]{:S(2)}) collective-permute-start(f32[3,8,153]{2,1,0:T(8,128)S(1)} %pad_maximum_fusion.3), channel_id=1, source_target_pairs={{0,4},{4,8},{8,12},{12,0},{1,5},{5,9},{9,13},{13,1},{2,6},{6,10},{... | collective-permute-start | bytes 44072 | tf_op jit(solution)/shard_map/ppermute | solution.py:20
  63.5 3.7 %collective-permute-start.11 = (f32[3,8,34]{2,1,0:T(8,128)S(1)}, f32[3,8,34]{2,1,0:T(8,128)S(1)}, u32[]{:S(2)}, u32[]{:S(2)}) collective-permute-start(f32[3,8,34]{2,1,0:T(8,128)S(1)} %pad_maximum_fusion.15), channel_id=1, source_target_pairs={{0,2},{2,0},{1,3},{3,1},{4,6},{6,4},{5,7},{7,5},{8,10},{10,8},{9,1... | collective-permute-start | bytes 9800 | tf_op jit(solution)/shard_map/ppermute | solution.py:20
  76.7 3.7 %collective-permute-start.12 = (f32[3,8,34]{2,1,0:T(8,128)S(1)}, f32[3,8,34]{2,1,0:T(8,128)S(1)}, u32[]{:S(2)}, u32[]{:S(2)}) collective-permute-start(f32[3,8,34]{2,1,0:T(8,128)S(1)} %pad_maximum_fusion.16), channel_id=1, source_target_pairs={{0,2},{2,0},{1,3},{3,1},{4,6},{6,4},{5,7},{7,5},{8,10},{10,8},{9,1... | collective-permute-start | bytes 9800 | tf_op jit(solution)/shard_map/ppermute | solution.py:20
  80.6 3.8 %collective-permute-start.13 = (f32[3,8,153]{2,1,0:T(8,128)S(1)}, f32[3,8,153]{2,1,0:T(8,128)S(1)}, u32[]{:S(2)}, u32[]{:S(2)}) collective-permute-start(f32[3,8,153]{2,1,0:T(8,128)S(1)} %pad_maximum_fusion.4), channel_id=1, source_target_pairs={{0,12},{4,0},{8,4},{12,8},{1,13},{5,1},{9,5},{13,9},{2,14},{6,2},{... | collective-permute-start | bytes 44072 | tf_op jit(solution)/shard_map/ppermute | solution.py:20
  84.6 1.2 collective-permute-start.14
  91.0 1.2 collective-permute-start.15
  92.4 5.6 %collective-permute-start.16 = (f32[3,8,153]{2,1,0:T(8,128)S(1)}, f32[3,8,153]{2,1,0:T(8,128)S(1)}, u32[]{:S(2)}, u32[]{:S(2)}) collective-permute-start(f32[3,8,153]{2,1,0:T(8,128)S(1)} %pad_maximum_fusion.5), channel_id=1, source_target_pairs={{0,4},{4,8},{8,12},{12,0},{1,5},{5,9},{9,13},{13,1},{2,6},{6,10},{... | collective-permute-start | bytes 44072 | tf_op jit(solution)/shard_map/ppermute | solution.py:20
  98.2 3.7 %collective-permute-start.17 = (f32[3,8,34]{2,1,0:T(8,128)S(1)}, f32[3,8,34]{2,1,0:T(8,128)S(1)}, u32[]{:S(2)}, u32[]{:S(2)}) collective-permute-start(f32[3,8,34]{2,1,0:T(8,128)S(1)} %pad_maximum_fusion.19), channel_id=1, source_target_pairs={{0,2},{2,0},{1,3},{3,1},{4,6},{6,4},{5,7},{7,5},{8,10},{10,8},{9,1... | collective-permute-start | bytes 9800 | tf_op jit(solution)/shard_map/ppermute | solution.py:20
  110.5 35.4 %copy-start.2 = (f32[3,8,128]{2,1,0:T(8,128)}, f32[3,8,128]{2,1,0:T(8,128)S(1)}, u32[]{:S(2)}) copy-start(f32[3,8,128]{2,1,0:T(8,128)S(1)} %pad_add_fusion) | copy-start | bytes 36868
  111.9 3.7 %collective-permute-start.18 = (f32[3,8,34]{2,1,0:T(8,128)S(1)}, f32[3,8,34]{2,1,0:T(8,128)S(1)}, u32[]{:S(2)}, u32[]{:S(2)}) collective-permute-start(f32[3,8,34]{2,1,0:T(8,128)S(1)} %pad_maximum_fusion.20), channel_id=1, source_target_pairs={{0,2},{2,0},{1,3},{3,1},{4,6},{6,4},{5,7},{7,5},{8,10},{10,8},{9,1... | collective-permute-start | bytes 9800 | tf_op jit(solution)/shard_map/ppermute | solution.py:20
  115.9 4.0 %collective-permute-start.19 = (f32[3,8,153]{2,1,0:T(8,128)S(1)}, f32[3,8,153]{2,1,0:T(8,128)S(1)}, u32[]{:S(2)}, u32[]{:S(2)}) collective-permute-start(f32[3,8,153]{2,1,0:T(8,128)S(1)} %pad_maximum_fusion.6), channel_id=1, source_target_pairs={{0,12},{4,0},{8,4},{12,8},{1,13},{5,1},{9,5},{13,9},{2,14},{6,2},{... | collective-permute-start | bytes 44072 | tf_op jit(solution)/shard_map/ppermute | solution.py:20
  120.1 1.2 collective-permute-start.20
  127.3 1.2 collective-permute-start.21
  128.8 5.6 %collective-permute-start.22 = (f32[3,8,153]{2,1,0:T(8,128)S(1)}, f32[3,8,153]{2,1,0:T(8,128)S(1)}, u32[]{:S(2)}, u32[]{:S(2)}) collective-permute-start(f32[3,8,153]{2,1,0:T(8,128)S(1)} %pad_maximum_fusion.7), channel_id=1, source_target_pairs={{0,4},{4,8},{8,12},{12,0},{1,5},{5,9},{9,13},{13,1},{2,6},{6,10},{... | collective-permute-start | bytes 44072 | tf_op jit(solution)/shard_map/ppermute | solution.py:20
  134.5 3.7 %collective-permute-start.23 = (f32[3,8,34]{2,1,0:T(8,128)S(1)}, f32[3,8,34]{2,1,0:T(8,128)S(1)}, u32[]{:S(2)}, u32[]{:S(2)}) collective-permute-start(f32[3,8,34]{2,1,0:T(8,128)S(1)} %pad_maximum_fusion.23), channel_id=1, source_target_pairs={{0,2},{2,0},{1,3},{3,1},{4,6},{6,4},{5,7},{7,5},{8,10},{10,8},{9,1... | collective-permute-start | bytes 9800 | tf_op jit(solution)/shard_map/ppermute | solution.py:20
